TPU v7x, 8 devices: a whole 2x2x1 slice. The times are simulated.
8 devices in a mesh: rep: 1 (over z), data: 2 (over y), expert: 4 (over x, core).
Axes of the slice: x: 2, y: 2, z: 1, core: 2. Of those that a mesh axis runs over, the one named last changes fastest.
Arguments:
- x_in: bfloat16 [2, 16384, 768], P(None, ('rep', 'expert', 'data'))
- expert_idx: int32 [2, 16384, 1], P(None, ('rep', 'expert', 'data'))
- gate_wt: float32 [2, 16384, 1], P(None, ('rep', 'expert', 'data'))
- w_gate: bfloat16 [8, 768, 3072], P('expert', 'data')
- w_up: bfloat16 [8, 768, 3072], P('expert', 'data')
- w_down: bfloat16 [8, 3072, 768], P('expert', None, 'data')
Outputs:
- output: bfloat16 [2, 16384, 768], P(None, ('rep', 'expert', 'data'))
All inputs are finite; a program needn't handle non-finite values.
Results may differ from a plain program's by a relative error of at most 0.001.
Values are sent between devices in bfloat16 or wider.
A program may use at most 1 GiB of HBM per device.

v0:
```python
import jax
import jax.numpy as jnp
from jax import lax
from jax.sharding import PartitionSpec as P, NamedSharding


def dispatch_block(x_blk, ids_blk, n_exp, capacity):
    tok_loc, n_top = ids_blk.shape
    pair_count = tok_loc * n_top
    slot_total = n_exp * capacity
    flat_ids = ids_blk.reshape(pair_count)
    one_hot = (flat_ids[:, None] == jnp.arange(n_exp, dtype=jnp.int32)[None, :]).astype(jnp.int32)
    slot_of = jnp.sum((jnp.cumsum(one_hot, axis=0) - one_hot) * one_hot, axis=1)
    is_kept = slot_of < capacity
    dest_pos = jnp.where(is_kept, flat_ids * capacity + slot_of, slot_total)
    source_of = jnp.full((slot_total,), pair_count, jnp.int32).at[dest_pos].set(jnp.arange(pair_count, dtype=jnp.int32), mode='drop')
    tok_of = jnp.minimum(source_of // n_top, tok_loc - 1)
    send_rows = jnp.where((source_of < pair_count)[:, None], jnp.take(x_blk, tok_of, axis=0), jnp.zeros((), x_blk.dtype))
    return send_rows, dest_pos, is_kept


def combine_block(x_blk, gate_blk, back_rows, dest_pos, is_kept):
    tok_loc, n_top = gate_blk.shape
    slot_total = back_rows.shape[0]
    pair_out = jnp.take(back_rows, jnp.minimum(dest_pos, slot_total - 1), axis=0).reshape(tok_loc, n_top, -1)
    weight = jnp.where(is_kept.reshape(tok_loc, n_top), gate_blk, 0.0)
    mix_sum = jnp.sum(pair_out.astype(jnp.float32) * weight[:, :, None], axis=1)
    return (x_blk.astype(jnp.float32) + mix_sum).astype(jnp.bfloat16)


def expert_mlp(rows_in, wg_full, wu_full, wd_full):
    gate_pre = jnp.einsum('lrd,ldf->lrf', rows_in, wg_full, preferred_element_type=jnp.float32)
    up_pre = jnp.einsum('lrd,ldf->lrf', rows_in, wu_full, preferred_element_type=jnp.float32)
    hidden = (jax.nn.silu(gate_pre) * up_pre).astype(jnp.bfloat16)
    return jnp.einsum('lrf,lfd->lrd', hidden, wd_full, preferred_element_type=jnp.float32).astype(jnp.bfloat16)


def solution(mesh):
    expert_devs = mesh.shape['expert']
    row_spec = P(None, ('rep', 'expert', 'data'), None)
    up_spec = P('expert', 'data', None)
    down_spec = P('expert', None, 'data')

    def per_device(x_loc, idx_loc, gate_loc, wg_loc, wu_loc, wd_loc):
        n_loc = wg_loc.shape[0]
        n_exp = n_loc * expert_devs
        d_model = x_loc.shape[2]
        tok_loc = idx_loc.shape[1]
        n_top = idx_loc.shape[2]
        capacity = 8 * ((5 * n_top * tok_loc + 32 * n_exp - 1) // (32 * n_exp))
        wg_full = lax.all_gather(wg_loc, 'data', axis=1, tiled=True)
        wu_full = lax.all_gather(wu_loc, 'data', axis=1, tiled=True)
        wd_full = lax.all_gather(wd_loc, 'data', axis=2, tiled=True)
        results = []
        for mb_index in range(x_loc.shape[0]):
            send_rows, dest_pos, is_kept = dispatch_block(x_loc[mb_index], idx_loc[mb_index], n_exp, capacity)
            recv_rows = lax.all_to_all(send_rows.reshape(expert_devs, n_loc, capacity, d_model), 'expert', 0, 2, tiled=True)
            out_rows = expert_mlp(recv_rows.reshape(n_loc, expert_devs * capacity, d_model), wg_full, wu_full, wd_full)
            back_rows = lax.all_to_all(out_rows.reshape(1, n_loc, expert_devs * capacity, d_model), 'expert', 2, 0, tiled=True)
            results.append(combine_block(x_loc[mb_index], gate_loc[mb_index], back_rows.reshape(n_exp * capacity, d_model), dest_pos, is_kept))
        return jnp.stack(results)

    return jax.shard_map(per_device, mesh=mesh, in_specs=(row_spec, row_spec, row_spec, up_spec, up_spec, down_spec), out_specs=row_spec, check_vma=False)
```

profile of v0, /device:TPU:1, one launch (start us, length us, event | category | flops | bytes accessed | tf_op | source)
XLA Modules:
  0.0 586.4 jit_solution(17227586478427295917)
XLA Ops:
  14.5 4.9 slice_bitcast_fusion.1
  20.1 8.1 %scatter_custom_fusion.1 = s32[2560]{0:T(1024)S(1)} fusion(s32[2048]{0:T(1024)S(1)} %bitcast.123, s32[2048]{0:T(1024)S(1)} %iota.20, s32[]{:T(128)} %constant.57.clone.1), kind=kCustom, calls=%fused_computation.60 | custom fusion | bytes 10244 | tf_op jit(solution)/shard_map/scatter | solution.py:16
  28.2 12.6 %gather_fusion.2 = bf16[2560,768]{1,0:T(8,128)(2,1)} fusion(bf16[2048,768]{1,0:T(8,128)(2,1)} %get-tuple-element.10, s32[3072]{0:T(1024)S(1)} %pad_clamp_fusion), kind=kCustom, calls=%fused_computation.2.clone | custom fusion | bytes 7874560 | tf_op jit(solution)/shard_map/jit(_take)/gather | solution.py:18
  45.4 4.8 all-to-all-start.2
  50.3 8.1 %scatter_custom_fusion = s32[2560]{0:T(1024)S(1)} fusion(s32[2048]{0:T(1024)S(1)} %bitcast.122, s32[2048]{0:T(1024)S(1)} %iota.19, s32[]{:T(128)} %constant.57.clone.1), kind=kCustom, calls=%fused_computation.63 | custom fusion | bytes 10244 | tf_op jit(solution)/shard_map/scatter | solution.py:16
  58.4 8.5 %gather_fusion = bf16[2560,768]{1,0:T(8,128)(2,1)} fusion(bf16[2048,768]{1,0:T(8,128)(2,1)S(1)} %get-tuple-element.9, s32[3072]{0:T(1024)S(1)} %pad_clamp_fusion.1), kind=kCustom, calls=%fused_computation.clone | custom fusion | bytes 7874560 | tf_op jit(solution)/shard_map/jit(_take)/gather | solution.py:18
  66.9 4.7 select_select_fusion.1
  71.6 23.3 %all-to-all-done.2 = bf16[4,2,320,768]{3,2,1,0:T(8,128)(2,1)} async-done(((bf16[4,2,320,768]{3,2,1,0:T(8,128)(2,1)}), bf16[4,2,320,768]{3,2,1,0:T(8,128)(2,1)}, u32[]{:S(2)}, u32[]{:S(2)}) %all-to-all-start.2) | async-done | bytes 3932192 | tf_op jit(solution)/shard_map/all_to_all | solution.py:57
  94.9 6.1 %all-to-all-start = ((bf16[4,2,320,768]{3,2,1,0:T(8,128)(2,1)}), bf16[4,2,320,768]{3,2,1,0:T(8,128)(2,1)}, u32[]{:S(2)}, u32[]{:S(2)}) async-start(bf16[4,2,320,768]{3,2,1,0:T(8,128)(2,1)} %bitcast.103), calls=%async_computation | async-start | bytes 7864320 | tf_op jit(solution)/shard_map/all_to_all | solution.py:57
  105.3 39.9 %all-to-all-done = bf16[4,2,320,768]{3,2,1,0:T(8,128)(2,1)} async-done(((bf16[4,2,320,768]{3,2,1,0:T(8,128)(2,1)}), bf16[4,2,320,768]{3,2,1,0:T(8,128)(2,1)}, u32[]{:S(2)}, u32[]{:S(2)}) %all-to-all-start) | async-done | bytes 3932192 | tf_op jit(solution)/shard_map/all_to_all | solution.py:57
  149.5 22.3 %fusion.27 = f32[2,1280,3072]{2,1,0:T(8,128)} fusion(bf16[2,1280,768]{2,1,0:T(8,128)(2,1)} %bitcast.106, bf16[2,768,3072]{2,1,0:T(8,128)(2,1)} %all-gather.4.cloned.1.call-done), kind=kOutput, calls=%fused_computation.76 | convolution fusion | flops 12079595520 | bytes 44826624 | tf_op jit(solution)/shard_map/lrd,ldf->lrf/dot_general | solution.py:32
  171.8 67.1 %all-gather.6.cloned.1.call-done = bf16[2,768,3072]{2,1,0:T(8,128)(2,1)} async-done(((bf16[2,384,3072]{2,1,0:T(8,128)(2,1)}), bf16[2,768,3072]{2,1,0:T(8,128)(2,1)}) %all-gather.6.cloned.1.call-update) | async-done | bytes 9437200 | tf_op jit(solution)/shard_map/all_gather | solution.py:52
  238.9 117.6 %all-gather.8.cloned.1.call-done = bf16[2,3072,768]{2,1,0:T(8,128)(2,1)} async-done(((bf16[2,3072,384]{2,1,0:T(8,128)(2,1)}), bf16[2,3072,768]{2,1,0:T(8,128)(2,1)}) %all-gather.8.cloned.1.call-update) | async-done | bytes 9437200 | tf_op jit(solution)/shard_map/all_gather | solution.py:53
  356.5 33.4 %fusion.9 = bf16[1,2,1280,768]{3,2,1,0:T(8,128)(2,1)} fusion(bf16[2,3072,768]{2,1,0:T(8,128)(2,1)} %all-gather.8.cloned.1.call-done, f32[2,1280,3072]{2,1,0:T(8,128)} %fusion.27, bf16[2,1280,768]{2,1,0:T(8,128)(2,1)} %bitcast.107, bf16[2,768,3072]{2,1,0:T(8,128)(2,1)} %all-gather.6.cloned.1.call-done), kind=kOutput, calls=%fused_computation.22 | convolution fusion | flops 24208343040 | bytes 58195968 | tf_op jit(solution)/shard_map/lrf,lfd->lrd/dot_general | solution.py:35
  390.0 21.4 %copy.19 = bf16[1,2,1280,768]{3,1,0,2:T(2,128)(2,1)} copy(bf16[1,2,1280,768]{3,2,1,0:T(8,128)(2,1)} %fusion.9) | data formatting | bytes 7864320 | tf_op jit(solution)/shard_map/reshape | solution.py:59
  411.3 5.7 all-to-all-start.3
  417.1 22.3 %fusion.26 = f32[2,1280,3072]{2,1,0:T(8,128)} fusion(bf16[2,1280,768]{2,1,0:T(8,128)(2,1)} %bitcast.104, bf16[2,768,3072]{2,1,0:T(8,128)(2,1)} %all-gather.4.cloned.1.call-done), kind=kOutput, calls=%fused_computation.75 | convolution fusion | flops 12079595520 | bytes 44826624 | tf_op jit(solution)/shard_map/lrd,ldf->lrf/dot_general | solution.py:32
  439.4 33.5 %fusion.8 = bf16[1,2,1280,768]{3,2,1,0:T(8,128)(2,1)} fusion(bf16[2,3072,768]{2,1,0:T(8,128)(2,1)} %all-gather.8.cloned.1.call-done, f32[2,1280,3072]{2,1,0:T(8,128)} %fusion.26, bf16[2,1280,768]{2,1,0:T(8,128)(2,1)} %bitcast.105, bf16[2,768,3072]{2,1,0:T(8,128)(2,1)} %all-gather.6.cloned.1.call-done), kind=kOutput, calls=%fused_computation.21 | convolution fusion | flops 24208343040 | bytes 58195968 | tf_op jit(solution)/shard_map/lrf,lfd->lrd/dot_general | solution.py:35
  472.9 21.4 %copy.16 = bf16[1,2,1280,768]{3,1,0,2:T(2,128)(2,1)} copy(bf16[1,2,1280,768]{3,2,1,0:T(8,128)(2,1)} %fusion.8) | data formatting | bytes 7864320 | tf_op jit(solution)/shard_map/reshape | solution.py:59
  494.3 5.0 all-to-all-start.1
  504.0 39.5 %all-to-all-done.1 = bf16[1,2,1280,768]{3,1,0,2:T(2,128)(2,1)} async-done(((bf16[1,2,1280,768]{3,1,0,2:T(2,128)(2,1)}), bf16[1,2,1280,768]{3,1,0,2:T(2,128)(2,1)}, u32[]{:S(2)}, u32[]{:S(2)}) %all-to-all-start.1) | async-done | bytes 3932192 | tf_op jit(solution)/shard_map/all_to_all | solution.py:59
  548.0 11.1 %gather_fusion.3 = bf16[2048,768]{1,0:T(8,128)(2,1)S(1)} fusion(bf16[2560,768]{1,0:T(8,128)(2,1)} %bitcast.100, s32[2048]{0:T(1024)S(1)} %broadcast_clamp_fusion), kind=kCustom, calls=%fused_computation.3.clone | custom fusion | bytes 6299648 | tf_op jit(solution)/shard_map/jit(_take)/gather | solution.py:25
  559.1 12.8 %gather_fusion.1 = bf16[2048,768]{1,0:T(8,128)(2,1)} fusion(bf16[2560,768]{1,0:T(8,128)(2,1)} %bitcast.101, s32[2048]{0:T(1024)S(1)} %broadcast_clamp_fusion.1), kind=kCustom, calls=%fused_computation.1.clone | custom fusion | bytes 6299648 | tf_op jit(solution)/shard_map/jit(_take)/gather | solution.py:25
  571.8 7.6 %fusion.5 = (bf16[2,2048,768]{2,1,0:T(8,128)(2,1)}, bf16[2,2048,768]{2,1,0:T(8,128)(2,1)}) fusion(bf16[2048,768]{1,0:T(8,128)(2,1)} %gather_fusion.1, f32[2048]{0:T(1024)S(1)} %get-tuple-element.24, pred[2048]{0:T(1024)(128)(4,1)S(1)} %get-tuple-element.22, bf16[2,2048,768]{2,1,0:T(8,128)(2,1)} %param.10, ...), kind=kLoop, output_to_operand_aliasing={{0}: (7, {}), {1}: (7, {})}, calls=%fused_computation.16 | loop fusion | flops 18874368 | bytes 18894848 | tf_op jit(solution)/shard_map/convert_element_type | solution.py:28
  (61 shorter events, 31.0 us)
Async XLA Ops:
  6.5 142.9 %all-gather.4.cloned.1.call-start = ((), (), s32[]{:S(2)}) async-start(), calls=%async_computation.4 | async-start | bytes 14155776 | tf_op jit(solution)/shard_map/all_gather | solution.py:51
  7.3 1.5 copy-start.8
  7.3 231.7 %all-gather.6.cloned.1.call-start = ((), (), s32[]{:S(2)}) async-start(), calls=%async_computation.5 | async-start | bytes 14155776 | tf_op jit(solution)/shard_map/all_gather | solution.py:52
  8.0 348.5 %all-gather.8.cloned.1.call-start = ((), (), s32[]{:S(2)}) async-start(), calls=%async_computation.6 | async-start | bytes 14155776 | tf_op jit(solution)/shard_map/all_gather | solution.py:53
  8.8 10.6 %copy-start.2 = (s32[1,2048,1]{1,2,0:T(1,128)}, s32[1,2048,1]{1,2,0:T(1,128)S(1)}, u32[]{:S(2)}) copy-start(s32[1,2048,1]{1,2,0:T(1,128)S(1)} %get-tuple-element.16) | copy-start | bytes 24580
  8.8 10.7 %copy-start = (s32[1,2048,1]{1,2,0:T(1,128)}, s32[1,2048,1]{1,2,0:T(1,128)S(1)}, u32[]{:S(2)}) copy-start(s32[1,2048,1]{1,2,0:T(1,128)S(1)} %get-tuple-element.15) | copy-start | bytes 24580
  19.4 0.6 copy-start.4
  19.5 21.3 %copy-start.6 = (s32[2048]{0:T(1024)}, s32[2048]{0:T(1024)S(1)}, u32[]{:S(2)}) copy-start(s32[2048]{0:T(1024)S(1)} %fusion.15) | copy-start | bytes 24580
  45.4 49.4 %all-to-all-start.2 = ((bf16[4,2,320,768]{3,2,1,0:T(8,128)(2,1)}), bf16[4,2,320,768]{3,2,1,0:T(8,128)(2,1)}, u32[]{:S(2)}, u32[]{:S(2)}) async-start(bf16[4,2,320,768]{3,2,1,0:T(8,128)(2,1)} %bitcast.102), calls=%async_computation.2 | async-start | bytes 7864320 | tf_op jit(solution)/shard_map/all_to_all | solution.py:57
  94.9 50.3 %all-to-all-start = ((bf16[4,2,320,768]{3,2,1,0:T(8,128)(2,1)}), bf16[4,2,320,768]{3,2,1,0:T(8,128)(2,1)}, u32[]{:S(2)}, u32[]{:S(2)}) async-start(bf16[4,2,320,768]{3,2,1,0:T(8,128)(2,1)} %bitcast.103), calls=%async_computation | async-start | bytes 7864320 | tf_op jit(solution)/shard_map/all_to_all | solution.py:57
  411.3 82.9 %all-to-all-start.3 = ((bf16[1,2,1280,768]{3,1,0,2:T(2,128)(2,1)}), bf16[1,2,1280,768]{3,1,0,2:T(2,128)(2,1)}, u32[]{:S(2)}, u32[]{:S(2)}) async-start(bf16[1,2,1280,768]{3,1,0,2:T(2,128)(2,1)} %copy.19), calls=%async_computation.3 | async-start | bytes 7864320 | tf_op jit(solution)/shard_map/all_to_all | solution.py:59
  494.2 5.0 copy-start.3
  494.2 5.0 copy-start.5
  494.2 5.0 copy-start.1
  494.2 5.0 copy-start.7
  494.2 5.1 copy-start.9
  494.3 49.2 %all-to-all-start.1 = ((bf16[1,2,1280,768]{3,1,0,2:T(2,128)(2,1)}), bf16[1,2,1280,768]{3,1,0,2:T(2,128)(2,1)}, u32[]{:S(2)}, u32[]{:S(2)}) async-start(bf16[1,2,1280,768]{3,1,0,2:T(2,128)(2,1)} %copy.16), calls=%async_computation.1 | async-start | bytes 7864320 | tf_op jit(solution)/shard_map/all_to_all | solution.py:59
Sparse Core Ops, SparseCore 0:
  8.8 115.0 all-gather.3
  125.5 113.4 all-gather.5
  240.5 116.0 all-gather.7
where the time goes:
time: 594 us; the launch traced here: 586 us
  waiting for transfers between devices  290 us (49%)
  local copies, waits for them, and re-layouts  128 us (22%)
  matrix products  112 us (19%)
  other arithmetic  22.3 us (4%)
  starting transfers between devices  21.7 us (4%)
  between operations  13.9 us (2%)
    all_gather x1, waiting for transfers between devices, per_device(): wd_full = lax.all_gather(wd_loc, 'data', axis=2, tiled=True)  118 us
    all_gather x1, waiting for transfers between devices, per_device(): wu_full = lax.all_gather(wu_loc, 'data', axis=1, tiled=True)  67.1 us
    dot_general x2, matrix products, expert_mlp(): jnp.einsum('lrf,lfd->lrd', hidden, wd_full, preferred_element_type=jnp.fl...  66.9 us
    all_to_all x2, waiting for transfers between devices, per_device(): lax.all_to_all(send_rows.reshape(expert_devs, n_loc, capacity, d_model),...  63.2 us
    dot_general x2, matrix products, expert_mlp(): jnp.einsum('lrd,ldf->lrf', rows_in, wg_full, preferred_element_type=jnp.f...  44.7 us
    reshape x2, local copies, waits for them, and re-layouts, per_device(): out_rows.reshape(1, n_loc, expert_devs * capacity, d_model)  42.7 us
    all_to_all x2, waiting for transfers between devices, per_device(): lax.all_to_all(out_rows.reshape(1, n_loc, expert_devs * capacity, d_model...  39.5 us
    gather x2, local copies, waits for them, and re-layouts, combine_block(): jnp.take(back_rows, jnp.minimum(dest_pos, slot_total - 1), axis=0)  23.8 us
  transfers between devices with their start and end apart: 7, of which 5 were waited for; matrix products, arithmetic and copies ran while one was open for 29% of the time, Pallas kernels for 0%

commit v1 on v0

v1 whole, which is shorter than its diff:
```python
import functools

import jax
import jax.numpy as jnp
from jax import lax
from jax.experimental import pallas as pl
from jax.experimental.pallas import tpu as pltpu
from jax.sharding import PartitionSpec as P

F32 = jnp.float32
BF16 = jnp.bfloat16
LANES = 128


def dot(a, b):
    return jnp.dot(a, b, preferred_element_type=F32)


def moe_kernel(dims, ids_ref, gate_ref, x_hbm, wg_hbm, wu_hbm, wd_hbm, y_hbm,
               xbuf, send, recv, back, oacc, wg_buf, wu_buf, wd_buf, p_buf, c_buf, slot_buf, cat_buf, col_buf,
               x_sem, y_sem, tok_send, tok_recv, ret_send, ret_recv, w_send, w_recv, w_loc, credit, go):
    cap, fc, nf = dims
    n_mb, tok, d_model = xbuf.shape
    half = d_model // 2
    groups = tok // LANES
    q_me = lax.axis_index('expert')
    y_me = lax.axis_index('data')
    x_me, c_me = lax.div(q_me, 2), lax.rem(q_me, 2)

    def piece(i):
        j = lax.div(i, 8)
        mb = lax.rem(lax.div(i, 4), 2)
        o = lax.rem(i, 4)
        hi = 1 - lax.div(o, 2)
        pp = lax.rem(o, 2)
        return j, mb, o, hi, pp

    def partner(hi, pp):
        return {'expert': lax.rem(x_me + hi, 2) * 2 + lax.rem(c_me + pp, 2)}

    def tok_copy(i):
        j, mb, o, hi, pp = piece(i)
        dst = recv.at[j, (1 - hi) * 2 + mb, pl.ds(pp * cap, cap), :]
        return pltpu.make_async_remote_copy(send.at[i], dst, tok_send.at[i], tok_recv.at[i], device_id=partner(hi, pp))

    def ret_copy(i):
        j, mb, o, hi, pp = piece(i)
        src = recv.at[j, (1 - hi) * 2 + mb, pl.ds(pp * cap, cap), :]
        dst = back.at[j, mb, pp, pl.ds(hi * cap, cap), :]
        return pltpu.make_async_remote_copy(src, dst, ret_send.at[i], ret_recv.at[i], device_id=partner(hi, pp))

    y_other = {'data': 1 - y_me}
    my_half = pl.ds(pl.multiple_of(y_me * half, half), half)

    def w_parts(j, k):
        cols = pl.ds(pl.multiple_of(k * fc, fc), fc)
        return ((wg_hbm.at[j, :, cols], wg_buf.at[k, my_half, :], 0),
                (wu_hbm.at[j, :, cols], wu_buf.at[k, my_half, :], 1),
                (wd_hbm.at[j, cols, :], wd_buf.at[k, :, my_half], 2))

    def w_remote(j, k):
        return [pltpu.make_async_remote_copy(s, d, w_send.at[k, n], w_recv.at[k, n], device_id=y_other)
                for s, d, n in w_parts(j, k)]

    def w_local(j, k):
        return [pltpu.make_async_copy(s, d, w_loc.at[k, n]) for s, d, n in w_parts(j, k)]

    barrier = pltpu.get_barrier_semaphore()
    for dev in (partner(0, 1), partner(1, 0), partner(1, 1), y_other):
        pl.semaphore_signal(barrier, inc=1, device_id=dev)
    pl.semaphore_wait(barrier, 4)

    def start_first(k, _):
        for c in w_remote(0, k):
            c.start()
        return 0

    @pl.when(c_me == 0)
    def _():
        lax.fori_loop(0, nf, start_first, 0)

    x_loads = [pltpu.make_async_copy(x_hbm.at[mb], xbuf.at[mb], x_sem.at[mb]) for mb in range(n_mb)]
    for c in x_loads:
        c.start()

    def start_local(k, _):
        for c in w_local(0, k):
            c.start()
        return 0

    lax.fori_loop(0, nf, start_local, 0)

    masks = []
    for mb in range(n_mb):
        ids = ids_ref[mb]
        for e in range(8):
            masks.append((ids == e).astype(F32))
    stack = jnp.concatenate(masks, axis=0).astype(BF16)
    rows = stack.shape[0]
    lane_r = lax.broadcasted_iota(jnp.int32, (LANES, LANES), 0)
    lane_c = lax.broadcasted_iota(jnp.int32, (LANES, LANES), 1)
    upper = jnp.where(lane_r < lane_c, 1.0, 0.0).astype(BF16)
    row_r = lax.broadcasted_iota(jnp.int32, (rows, rows), 0)
    row_c = lax.broadcasted_iota(jnp.int32, (rows, rows), 1)
    first = row_r - lax.rem(row_r, groups)
    lower = jnp.where((row_c >= first) & (row_c < row_r), 1.0, 0.0).astype(BF16)
    ones = jnp.ones((LANES, LANES), BF16)
    prefix = dot(stack, upper) + dot(dot(lower, stack).astype(BF16), ones)
    cat_buf[...] = jnp.zeros_like(cat_buf)
    for mb in range(n_mb):
        place = jnp.full((groups, LANES), -1.0, F32)
        for e in range(8):
            r0 = (mb * 8 + e) * groups
            slot = prefix[r0:r0 + groups]
            j, qe = e % 2, e // 2
            hi = lax.rem(x_me + qe // 2, 2)
            pp = lax.rem(c_me + qe % 2, 2)
            base = (((j * 2 + pp) * 2 + hi) * cap).astype(F32)
            place = jnp.where((masks[mb * 8 + e] > 0.5) & (slot < float(cap)), base + slot, place)
        slot_buf[mb] = place
        cat_buf[mb, 0:groups, :] = place
        cat_buf[mb, groups:2 * groups, :] = gate_ref[mb]
        col_buf[mb] = cat_buf[mb].T

    for c in x_loads:
        c.wait()

    def dispatch(i, _):
        j, mb, o, hi, pp = piece(i)
        base = (((j * 2 + pp) * 2 + hi) * cap).astype(F32)
        want = lax.broadcasted_iota(jnp.int32, (cap, LANES), 0).astype(F32) + base
        place = slot_buf[mb]
        for g in range(groups):
            p_buf[:, g * LANES:(g + 1) * LANES] = jnp.where(place[g:g + 1, :] == want, 1.0, 0.0).astype(BF16)
        out = dot(p_buf[...], xbuf[mb]).astype(BF16)

        @pl.when(o == 2)
        def _():
            recv[j, 2 + mb, 0:cap, :] = out

        @pl.when(o != 2)
        def _():
            send[i] = out

        @pl.when((i > 0) & (o != 3))
        def _():
            tok_copy(i - 1).start()

        return 0

    lax.fori_loop(0, 16, dispatch, 0)
    tok_copy(15).start()

    @pl.when(c_me == 1)
    def _():
        pl.semaphore_wait(go, 1)
        lax.fori_loop(0, nf, start_first, 0)

    def wait_tokens(j):
        for r in range(8):
            if r % 4 != 2:
                tok_copy(j * 8 + r).wait_recv()

    def wait_weights(j, k):
        for c in w_local(j, k):
            c.wait()
        for c in w_remote(j, k):
            c.wait()

    def hidden_times_down(rows_in, k):
        gate_pre = dot(rows_in, wg_buf[k])
        up_pre = dot(rows_in, wu_buf[k])
        hidden = (gate_pre / (1.0 + jnp.exp(-gate_pre)) * up_pre).astype(BF16)
        return dot(hidden, wd_buf[k])

    def expert(j):
        oacc[...] = jnp.zeros_like(oacc)
        wait_tokens(j)

        def chunk(k, _):
            wait_weights(j, k)

            def block(b, _):
                oacc[b] += hidden_times_down(recv[j, b], k)
                return 0

            lax.fori_loop(0, 4, block, 0)
            if j == 0:
                pl.semaphore_signal(credit, inc=1, device_id=y_other)
                pl.semaphore_wait(credit, 1)
                for c in w_remote(1, k) + w_local(1, k):
                    c.start()
            else:
                @pl.when((k == nf - 3) & (c_me == 0))
                def _():
                    pl.semaphore_signal(go, inc=1, device_id=partner(0, 1))
            return 0

        lax.fori_loop(0, nf - 1, chunk, 0)
        last = nf - 1
        wait_weights(j, last)

        def index_of(r):
            b, pp = lax.div(r, 2), lax.rem(r, 2)
            return j * 8 + lax.rem(b, 2) * 4 + lax.div(b, 2) * 2 + pp

        def finish(r, _):
            b, pp = lax.div(r, 2), lax.rem(r, 2)
            rows_at = pl.ds(pl.multiple_of(pp * cap, cap), cap)
            res = (oacc[b, rows_at, :] + hidden_times_down(recv[j, b, rows_at, :], last)).astype(BF16)
            own = (b >= 2) & (pp == 0)

            @pl.when(own)
            def _():
                back[j, lax.rem(b, 2), 0, 0:cap, :] = res

            @pl.when(jnp.logical_not(own))
            def _():
                recv[j, b, rows_at, :] = res

            @pl.when((r > 0) & (r != 5) & (r != 7))
            def _():
                ret_copy(index_of(r - 1)).start()

            return 0

        lax.fori_loop(0, 8, finish, 0)
        ret_copy(index_of(7)).start()
        if j == 0:
            pl.semaphore_signal(credit, inc=1, device_id=y_other)
            pl.semaphore_wait(credit, 1)
            for c in w_remote(1, last) + w_local(1, last):
                c.start()

    def combine(j, pp, mb):
        i = j * 8 + mb * 4 + pp
        ret_copy(i).wait_recv()

        @pl.when(pp == 1)
        def _():
            ret_copy(i + 2).wait_recv()

        base = ((j * 2 + pp) * 2 * cap).astype(F32)
        want = lax.broadcasted_iota(jnp.int32, (LANES, 2 * cap), 1).astype(F32) + base
        for g in range(groups):
            c_buf[g * LANES:(g + 1) * LANES, :] = jnp.where(col_buf[mb, :, g:g + 1] == want, 1.0, 0.0).astype(BF16)
        for blk in range(4):
            size = tok // 4
            picked = dot(c_buf[blk * size:(blk + 1) * size, :], back[j, mb, pp])
            for s in range(size // LANES):
                g = blk * (size // LANES) + s
                at = slice(g * LANES, (g + 1) * LANES)
                gate = col_buf[mb, :, groups + g:groups + g + 1]
                part = picked[s * LANES:(s + 1) * LANES, :]
                xbuf[mb, at, :] = (xbuf[mb, at, :].astype(F32) + gate * part).astype(BF16)

    def combine_step(n, pp):
        combine(lax.rem(lax.div(n, 2), 2), pp, lax.rem(n, 2))

    expert(0)

    def early(n, _):
        combine_step(n, jnp.int32(1))
        return 0

    lax.fori_loop(0, 4 * c_me, early, 0)
    expert(1)

    def late(n, _):
        combine_step(n, lax.div(n, 4))
        return 0

    total = 8 - 4 * c_me
    lax.fori_loop(0, total - 1, late, 0)
    outs = [pltpu.make_async_copy(xbuf.at[mb], y_hbm.at[mb], y_sem.at[mb]) for mb in range(n_mb)]
    outs[0].start()
    late(total - 1, 0)
    outs[1].start()

    for i in range(16):
        if i % 4 != 2:
            tok_copy(i).wait_send()
            ret_copy(i).wait_send()
    for c in outs:
        c.wait()


def solution(mesh):
    row_spec = P(None, ('rep', 'expert', 'data'), None)
    up_spec = P('expert', 'data', None)
    down_spec = P('expert', None, 'data')

    def per_device(x_loc, idx_loc, gate_loc, wg_loc, wu_loc, wd_loc):
        n_mb, tok, d_model = x_loc.shape
        n_loc, half, ff = wg_loc.shape
        n_exp = n_loc * mesh.shape['expert']
        n_top = idx_loc.shape[2]
        assert n_top == 1 and n_exp == 8 and n_mb == 2
        cap = 8 * ((5 * n_top * tok + 32 * n_exp - 1) // (32 * n_exp))
        fc = 256
        nf = ff // fc
        groups = tok // LANES
        hbm = pl.BlockSpec(memory_space=pl.ANY)
        vmem = pl.BlockSpec(memory_space=pltpu.VMEM)
        dma = pltpu.SemaphoreType.DMA
        return pl.pallas_call(
            functools.partial(moe_kernel, (cap, fc, nf)),
            out_shape=jax.ShapeDtypeStruct(x_loc.shape, BF16),
            in_specs=[vmem, vmem, hbm, hbm, hbm, hbm],
            out_specs=hbm,
            scratch_shapes=[
                pltpu.VMEM((n_mb, tok, d_model), BF16),
                pltpu.VMEM((16, cap, d_model), BF16),
                pltpu.VMEM((2, 4, 2 * cap, d_model), BF16),
                pltpu.VMEM((2, n_mb, 2, 2 * cap, d_model), BF16),
                pltpu.VMEM((4, 2 * cap, d_model), F32),
                pltpu.VMEM((nf, d_model, fc), BF16),
                pltpu.VMEM((nf, d_model, fc), BF16),
                pltpu.VMEM((nf, fc, d_model), BF16),
                pltpu.VMEM((cap, tok), BF16),
                pltpu.VMEM((tok, 2 * cap), BF16),
                pltpu.VMEM((n_mb, groups, LANES), F32),
                pltpu.VMEM((n_mb, LANES, LANES), F32),
                pltpu.VMEM((n_mb, LANES, LANES), F32),
                dma((n_mb,)), dma((n_mb,)),
                dma((16,)), dma((16,)), dma((16,)), dma((16,)),
                dma((nf, 3)), dma((nf, 3)), dma((nf, 3)),
                pltpu.SemaphoreType.REGULAR, pltpu.SemaphoreType.REGULAR,
            ],
            compiler_params=pltpu.CompilerParams(
                collective_id=0, has_side_effects=True, vmem_limit_bytes=64 * 1024 * 1024 - 65536),
        )(idx_loc.reshape(n_mb, groups, LANES), gate_loc.reshape(n_mb, groups, LANES), x_loc, wg_loc, wu_loc, wd_loc)

    return jax.shard_map(per_device, mesh=mesh, in_specs=(row_spec, row_spec, row_spec, up_spec, up_spec, down_spec),
                         out_specs=row_spec, check_vma=False)
```

time: 594 us -> 352 us (0.59)
  Pallas kernels: 0 us -> 339 us
  waiting for transfers between devices: 290 us -> 0 us
  local copies, waits for them, and re-layouts: 128 us -> 5.89 us
  matrix products: 112 us -> 0 us
  other arithmetic: 22.3 us -> 0 us
  starting transfers between devices: 21.7 us -> 0 us
  between operations: 13.9 us -> 0.01 us
    pallas_call x0 -> x1, Pallas kernels: none -> 339 us  [per_device(): pl.pallas_call(functools.partial(moe_kernel, (cap, fc, nf)), out_shape=ja...]
    all_gather x3 -> x0, waiting for transfers between devices: 185 us -> none  [the longest x1 118 us: per_device(): wd_full = lax.all_gather(wd_loc, 'data', axis=2, tiled=True)]
    dot_general x4 -> x0, matrix products: 112 us -> none  [the longest x2 66.9 us: expert_mlp(): jnp.einsum('lrf,lfd->lrd', hidden, wd_full, preferred_element_type=jnp.fl...]
    all_to_all x4 -> x0, waiting for transfers between devices: 103 us -> none  [the longest x2 63.2 us: per_device(): lax.all_to_all(send_rows.reshape(expert_devs, n_loc, capacity, d_model),...]
    gather x4 -> x0, local copies, waits for them, and re-layouts: 44.9 us -> none  [the longest x2 23.8 us: combine_block(): jnp.take(back_rows, jnp.minimum(dest_pos, slot_total - 1), axis=0)]
    reshape x2 -> x0, local copies, waits for them, and re-layouts: 42.7 us -> none  [per_device(): out_rows.reshape(1, n_loc, expert_devs * capacity, d_model)]
    all_to_all x4 -> x0, starting transfers between devices: 21.6 us -> none  [the longest x2 10.9 us: per_device(): lax.all_to_all(send_rows.reshape(expert_devs, n_loc, capacity, d_model),...]
    all_to_all x4 -> x0, local copies, waits for them, and re-layouts: 17.7 us -> none  [the longest x2 9.12 us: per_device(): lax.all_to_all(out_rows.reshape(1, n_loc, expert_devs * capacity, d_model...]
  transfers between devices with their start and end apart: 7 -> 0, of which waited for: 5 -> 0; matrix products, arithmetic and copies ran while one was open for 29% -> 0% of each run, Pallas kernels for 0% -> 0%
where the time goes in v1:
time: 352 us; the launch traced here: 345 us
  Pallas kernels  339 us (96%)
  local copies, waits for them, and re-layouts  5.89 us (2%)
    pallas_call x1, Pallas kernels, per_device(): pl.pallas_call(functools.partial(moe_kernel, (cap, fc, nf)), out_shape=ja...  339 us

profile of v1, /device:TPU:1, one launch (start us, length us, event | category | flops | bytes accessed | tf_op | source)
XLA Modules:
  0.0 345.2 jit_solution(2471922734592142725)
XLA Ops:
  0.0 339.3 %shard_map.64 = bf16[2,2048,768]{2,1,0:T(8,128)(2,1)} custom-call(s32[2,16,128]{2,1,0:T(8,128)} %bitcast.2, f32[2,16,128]{2,1,0:T(8,128)} %bitcast.3, bf16[2,2048,768]{2,1,0:T(8,128)(2,1)} %x_hbm.1, bf16[2,384,3072]{2,1,0:T(8,128)(2,1)} %wg_hbm.1, bf16[2,384,3072]{2,1,0:T(8,128)(2,1)} %wu_hbm.1, bf16[2,3072,384]{2,1,0:T(8,128)(2,1)} %wd_hbm.1), custom_call_target="tpu_custom_call" | custom-call | tf_op jit(solution)/shard_map/pallas_call | solution.py:306
  339.3 5.9 %copy.8 = bf16[2,2048,768]{2,1,0:T(8,128)(2,1)} copy(bf16[2,2048,768]{2,1,0:T(8,128)(2,1)} %shard_map.64) | data formatting | bytes 12582912

commit v2 on v1

v2 whole, which is shorter than its diff:
```python
import functools

import jax
import jax.numpy as jnp
from jax import lax
from jax.experimental import pallas as pl
from jax.experimental.pallas import tpu as pltpu
from jax.sharding import PartitionSpec as P

F32 = jnp.float32
BF16 = jnp.bfloat16
LANES = 128


def dot(a, b):
    return jnp.dot(a, b, preferred_element_type=F32)


def moe_kernel(dims, ids_ref, gate_ref, x_hbm, wg_hbm, wu_hbm, wd_hbm, y_hbm,
               xbuf, send, recv, back, oacc, wg_buf, wu_buf, wd_buf, p_buf, c_buf, slot_buf, cat_buf, col_buf,
               x_sem, y_sem, tok_send, tok_recv, ret_send, ret_recv, w_send, w_recv, w_loc, credit, go):
    cap, fc, nf, early = dims
    n_mb, tok, d_model = xbuf.shape
    half = d_model // 2
    groups = tok // LANES
    q_me = lax.axis_index('expert')
    y_me = lax.axis_index('data')
    x_me, c_me = lax.div(q_me, 2), lax.rem(q_me, 2)
    is_a = c_me == 0
    is_b = c_me == 1

    def device(dx, dy, c):
        return {'expert': lax.rem(x_me + dx, 2) * 2 + c, 'data': lax.rem(y_me + dy, 2)}

    def piece(i):
        g = lax.div(i, 4)
        hi = 1 - lax.div(lax.rem(i, 4), 2)
        return g, hi, lax.rem(i, 2)

    def home_own(i):
        g, hi, _ = piece(i)
        return (hi == 0) & (((g >= 2) & is_a) | ((g == 1) & is_b))

    def slot_own(b, sub):
        hi = 1 - lax.div(lax.rem(b, 4), 2)
        return (hi == 0) & (sub == c_me) & (is_a | (b >= 4))

    def part(sub):
        return pl.ds(pl.multiple_of(sub * cap, cap), cap)

    def tok_copy(i):
        g, hi, mb = piece(i)
        dev = device(hi, jnp.where(g == 0, 1, 0), jnp.where(g >= 2, 0, 1))
        b = lax.rem(i, 8)
        return pltpu.make_async_remote_copy(send.at[i], recv.at[b, part(c_me), :], tok_send.at[i],
                                            tok_recv.at[b * 2 + c_me], device_id=dev)

    def tok_arrival(b, sub):
        return pltpu.make_async_remote_copy(send.at[0], recv.at[b, part(sub), :], tok_send.at[0],
                                            tok_recv.at[b * 2 + sub], device_id=device(1, 0, 0))

    def ret_copy(b, sub):
        g = (1 - c_me) * 2 + lax.div(b, 4)
        hi = 1 - lax.div(lax.rem(b, 4), 2)
        mb = lax.rem(b, 2)
        dev = device(hi, jnp.where(g == 0, 1, 0), sub)
        i = (1 - c_me) * 8 + b
        return pltpu.make_async_remote_copy(recv.at[b, part(sub), :], back.at[g, mb, part(hi), :],
                                            ret_send.at[b * 2 + sub], ret_recv.at[i], device_id=dev)

    def ret_arrival(i):
        g, hi, mb = piece(i)
        return pltpu.make_async_remote_copy(send.at[0], back.at[g, mb, part(hi), :], ret_send.at[0],
                                            ret_recv.at[i], device_id=device(1, 0, 0))

    y_other = {'data': 1 - y_me}
    my_half = pl.ds(pl.multiple_of(y_me * half, half), half)

    def w_parts(j, k):
        cols = pl.ds(pl.multiple_of(k * fc, fc), fc)
        return ((wg_hbm.at[j, :, cols], wg_buf.at[k, my_half, :], 0),
                (wu_hbm.at[j, :, cols], wu_buf.at[k, my_half, :], 1),
                (wd_hbm.at[j, cols, :], wd_buf.at[k, :, my_half], 2))

    def w_remote(j, k):
        return [pltpu.make_async_remote_copy(s, d, w_send.at[k, n], w_recv.at[k, n], device_id=y_other)
                for s, d, n in w_parts(j, k)]

    def w_local(j, k):
        return [pltpu.make_async_copy(s, d, w_loc.at[k, n]) for s, d, n in w_parts(j, k)]

    barrier = pltpu.get_barrier_semaphore()
    for n in range(1, 8):
        other = device(n // 4, (n // 2) % 2, lax.rem(c_me + n % 2, 2))
        pl.semaphore_signal(barrier, inc=1, device_id=other)
    pl.semaphore_wait(barrier, 7)

    j_out = jnp.where(is_a, 0, 1 - y_me)
    j_in = jnp.where(is_a, 0, y_me)

    def start_remote(k, _):
        for c in w_remote(j_out, k):
            c.start()
        return 0

    def start_local(k, _):
        for c in w_local(j_in, k):
            c.start()
        return 0

    lax.fori_loop(0, early * c_me, start_remote, 0)
    x_loads = [pltpu.make_async_copy(x_hbm.at[mb], xbuf.at[mb], x_sem.at[mb]) for mb in range(n_mb)]
    for c in x_loads:
        c.start()
    lax.fori_loop(0, nf, start_local, 0)

    masks = []
    for mb in range(n_mb):
        ids = ids_ref[mb]
        for e in range(8):
            masks.append((ids == e).astype(F32))
    stack = jnp.concatenate(masks, axis=0).astype(BF16)
    rows = stack.shape[0]
    lane_r = lax.broadcasted_iota(jnp.int32, (LANES, LANES), 0)
    lane_c = lax.broadcasted_iota(jnp.int32, (LANES, LANES), 1)
    upper = jnp.where(lane_r < lane_c, 1.0, 0.0).astype(BF16)
    row_r = lax.broadcasted_iota(jnp.int32, (rows, rows), 0)
    row_c = lax.broadcasted_iota(jnp.int32, (rows, rows), 1)
    first = row_r - lax.rem(row_r, groups)
    lower = jnp.where((row_c >= first) & (row_c < row_r), 1.0, 0.0).astype(BF16)
    ones = jnp.ones((LANES, LANES), BF16)
    prefix = dot(stack, upper) + dot(dot(lower, stack).astype(BF16), ones)
    cat_buf[...] = jnp.zeros_like(cat_buf)
    for mb in range(n_mb):
        place = jnp.full((groups, LANES), -1.0, F32)
        for e in range(8):
            r0 = (mb * 8 + e) * groups
            slot = prefix[r0:r0 + groups]
            x_e, c_e, j = e // 4, (e // 2) % 2, e % 2
            hi = lax.rem(x_me + x_e, 2)
            g = 1 - lax.rem(y_me + j, 2) if c_e else 2 + j
            base = ((g * 2 + hi) * cap).astype(F32)
            place = jnp.where((masks[mb * 8 + e] > 0.5) & (slot < float(cap)), base + slot, place)
        slot_buf[mb] = place
        cat_buf[mb, 0:groups, :] = place
        cat_buf[mb, groups:2 * groups, :] = gate_ref[mb]
        col_buf[mb] = cat_buf[mb].T

    for c in x_loads:
        c.wait()

    def dispatch(i, _):
        g, hi, mb = piece(i)
        base = ((g * 2 + hi) * cap).astype(F32)
        want = lax.broadcasted_iota(jnp.int32, (cap, LANES), 0).astype(F32) + base
        place = slot_buf[mb]
        for n in range(groups):
            p_buf[:, n * LANES:(n + 1) * LANES] = jnp.where(place[n:n + 1, :] == want, 1.0, 0.0).astype(BF16)
        out = dot(p_buf[...], xbuf[mb]).astype(BF16)
        own = home_own(i)

        @pl.when(own)
        def _():
            recv[lax.rem(i, 8), part(c_me), :] = out

        @pl.when(jnp.logical_not(own))
        def _():
            send[i] = out

        @pl.when((i > 0) & jnp.logical_not(home_own(i - 1)))
        def _():
            tok_copy(i - 1).start()

        return 0

    lax.fori_loop(0, 16, dispatch, 0)

    @pl.when(is_b)
    def _():
        tok_copy(15).start()

    def wait_tokens(b, _):
        for sub in range(2):
            @pl.when(jnp.logical_not(slot_own(b, sub)))
            def _():
                tok_arrival(b, sub).wait_recv()
        return 0

    def wait_weights(k):
        for c in w_local(0, k):
            c.wait()
        for c in w_remote(0, k):
            c.wait()

    def ffn(rows_in, k):
        gate_pre = dot(rows_in, wg_buf[k])
        up_pre = dot(rows_in, wu_buf[k])
        hidden = (gate_pre / (1.0 + jnp.exp(-gate_pre)) * up_pre).astype(BF16)
        return dot(hidden, wd_buf[k])

    def clear(b, _):
        oacc[b] = jnp.zeros_like(oacc[b])
        return 0

    def add_chunk(k, lo, hi):
        def block(b, _):
            oacc[b] += ffn(recv[b], k)
            return 0

        lax.fori_loop(lo, hi, block, 0)

    def finish(lo, hi):
        last = nf - 1

        def one(r, _):
            b, sub = lax.div(r, 2), lax.rem(r, 2)
            res = (oacc[b, part(sub), :] + ffn(recv[b, part(sub), :], last)).astype(BF16)
            own = slot_own(b, sub)

            @pl.when(own)
            def _():
                back[(1 - c_me) * 2 + lax.div(b, 4), lax.rem(b, 2), 0:cap, :] = res

            @pl.when(jnp.logical_not(own))
            def _():
                recv[b, part(sub), :] = res

            before = r - 1

            @pl.when((r > lo * 2) & jnp.logical_not(slot_own(lax.div(before, 2), lax.rem(before, 2))))
            def _():
                ret_copy(lax.div(before, 2), lax.rem(before, 2)).start()

            return 0

        lax.fori_loop(lo * 2, hi * 2, one, 0)

    def combine(g, mb):
        for hi in range(2):
            i = g * 4 + (1 - hi) * 2 + mb

            @pl.when(jnp.logical_not(home_own(i)))
            def _():
                ret_arrival(i).wait_recv()

        want = lax.broadcasted_iota(jnp.int32, (LANES, 2 * cap), 1).astype(F32) + (g * 2 * cap).astype(F32)
        size = c_buf.shape[0]
        for blk in range(tok // size):
            for s in range(size // LANES):
                n = blk * (size // LANES) + s
                c_buf[s * LANES:(s + 1) * LANES, :] = jnp.where(col_buf[mb, :, n:n + 1] == want, 1.0, 0.0).astype(BF16)
            picked = dot(c_buf[...], back[g, mb])
            for s in range(size // LANES):
                n = blk * (size // LANES) + s
                at = slice(n * LANES, (n + 1) * LANES)
                gate = col_buf[mb, :, groups + n:groups + n + 1]
                xbuf[mb, at, :] = (xbuf[mb, at, :].astype(F32) + gate * picked[s * LANES:(s + 1) * LANES, :]).astype(BF16)

    @pl.when(is_a)
    def _():
        pl.semaphore_wait(go, 1)
        lax.fori_loop(0, nf, start_remote, 0)

        def expert(j, _):
            lo, hi = j * 4, j * 4 + 4
            lax.fori_loop(lo, hi, clear, 0)
            lax.fori_loop(lo, hi, wait_tokens, 0)

            def refill(k):
                @pl.when(j == 0)
                def _():
                    pl.semaphore_signal(credit, inc=1, device_id=y_other)
                    pl.semaphore_wait(credit, 1)
                    for c in w_remote(1, k) + w_local(1, k):
                        c.start()

            def chunk(k, _):
                wait_weights(k)
                add_chunk(k, lo, hi)
                refill(k)

                @pl.when((k == nf - 3) & (j == 1))
                def _():
                    pl.semaphore_signal(go, inc=1, device_id=device(0, 0, 1))

                return 0

            lax.fori_loop(0, nf - 1, chunk, 0)
            wait_weights(nf - 1)
            finish(lo, hi)
            ret_copy(hi - 1, 1).start()
            refill(nf - 1)
            return 0

        lax.fori_loop(0, 2, expert, 0)

    def combine_both(g):
        def step(mb, _):
            combine(g, mb)
            return 0

        lax.fori_loop(0, n_mb, step, 0)

    @pl.when(is_b)
    def _():
        for c in w_remote(j_out, early - 3):
            c.wait_send()
        pl.semaphore_signal(go, inc=1, device_id=device(0, 0, 0))
        lax.fori_loop(0, 8, clear, 0)
        lax.fori_loop(0, 8, wait_tokens, 0)

        def chunk(k, _):
            for c in w_local(0, k):
                c.wait()
            for c in w_remote(0, k):
                c.wait_recv()

            @pl.when(k != early - 3)
            def _():
                for c in w_remote(0, k):
                    c.wait_send()

            @pl.when(k < nf - 1)
            def _():
                add_chunk(k, 0, 8)

            @pl.when(k == early - 1)
            def _():
                combine_both(jnp.int32(2))
                pl.semaphore_wait(go, 1)
                lax.fori_loop(early, nf, start_remote, 0)

            return 0

        lax.fori_loop(0, nf, chunk, 0)
        finish(0, 8)

    def late(n, _):
        g = lax.rem(lax.div(n, 2) + 2, 4)
        combine(g, lax.rem(n, 2))
        return 0

    lax.fori_loop(2 * c_me, 7, late, 0)
    outs = [pltpu.make_async_copy(xbuf.at[mb], y_hbm.at[mb], y_sem.at[mb]) for mb in range(n_mb)]
    outs[0].start()
    late(jnp.int32(7), 0)
    outs[1].start()

    def drain(i, _):
        @pl.when(jnp.logical_not(home_own(i)))
        def _():
            tok_copy(i).wait_send()

        b, sub = lax.div(i, 2), lax.rem(i, 2)

        @pl.when(jnp.logical_not(slot_own(b, sub)))
        def _():
            ret_copy(b, sub).wait_send()

        return 0

    lax.fori_loop(0, 16, drain, 0)
    for c in outs:
        c.wait()


def solution(mesh):
    row_spec = P(None, ('rep', 'expert', 'data'), None)
    up_spec = P('expert', 'data', None)
    down_spec = P('expert', None, 'data')

    def per_device(x_loc, idx_loc, gate_loc, wg_loc, wu_loc, wd_loc):
        n_mb, tok, d_model = x_loc.shape
        n_loc, half, ff = wg_loc.shape
        n_exp = n_loc * mesh.shape['expert']
        n_top = idx_loc.shape[2]
        assert n_top == 1 and n_exp == 8 and n_mb == 2
        cap = 8 * ((5 * n_top * tok + 32 * n_exp - 1) // (32 * n_exp))
        fc = 256
        nf = ff // fc
        early = 9
        groups = tok // LANES
        hbm = pl.BlockSpec(memory_space=pl.ANY)
        vmem = pl.BlockSpec(memory_space=pltpu.VMEM)
        dma = pltpu.SemaphoreType.DMA
        return pl.pallas_call(
            functools.partial(moe_kernel, (cap, fc, nf, early)),
            out_shape=jax.ShapeDtypeStruct(x_loc.shape, BF16),
            in_specs=[vmem, vmem, hbm, hbm, hbm, hbm],
            out_specs=hbm,
            scratch_shapes=[
                pltpu.VMEM((n_mb, tok, d_model), BF16),
                pltpu.VMEM((16, cap, d_model), BF16),
                pltpu.VMEM((8, 2 * cap, d_model), BF16),
                pltpu.VMEM((4, n_mb, 2 * cap, d_model), BF16),
                pltpu.VMEM((8, 2 * cap, d_model), F32),
                pltpu.VMEM((nf, d_model, fc), BF16),
                pltpu.VMEM((nf, d_model, fc), BF16),
                pltpu.VMEM((nf, fc, d_model), BF16),
                pltpu.VMEM((cap, tok), BF16),
                pltpu.VMEM((512, 2 * cap), BF16),
                pltpu.VMEM((n_mb, groups, LANES), F32),
                pltpu.VMEM((n_mb, LANES, LANES), F32),
                pltpu.VMEM((n_mb, LANES, LANES), F32),
                dma((n_mb,)), dma((n_mb,)),
                dma((16,)), dma((16,)), dma((16,)), dma((16,)),
                dma((nf, 3)), dma((nf, 3)), dma((nf, 3)),
                pltpu.SemaphoreType.REGULAR, pltpu.SemaphoreType.REGULAR,
            ],
            compiler_params=pltpu.CompilerParams(
                collective_id=0, has_side_effects=True, vmem_limit_bytes=64 * 1024 * 1024 - 65536),
        )(idx_loc.reshape(n_mb, groups, LANES), gate_loc.reshape(n_mb, groups, LANES), x_loc, wg_loc, wu_loc, wd_loc)

    return jax.shard_map(per_device, mesh=mesh, in_specs=(row_spec, row_spec, row_spec, up_spec, up_spec, down_spec),
                         out_specs=row_spec, check_vma=False)
```

time: 352 us -> 345 us (0.980); the launches traced: 345 us -> 345 us
  no operation moved by 1% of the time
where the time goes in v2:
time: 345 us
  Pallas kernels  339 us (98%)
  local copies, waits for them, and re-layouts  5.89 us (2%)
    pallas_call x1, Pallas kernels, per_device(): pl.pallas_call(functools.partial(moe_kernel, (cap, fc, nf, early)), out_s...  339 us

profile of v2, /device:TPU:1, one launch (start us, length us, event | category | flops | bytes accessed | tf_op | source)
XLA Modules:
  0.0 344.9 jit_solution(10412818049252291771)
XLA Ops:
  0.0 338.9 %shard_map.64 = bf16[2,2048,768]{2,1,0:T(8,128)(2,1)} custom-call(s32[2,16,128]{2,1,0:T(8,128)} %bitcast.2, f32[2,16,128]{2,1,0:T(8,128)} %bitcast.3, bf16[2,2048,768]{2,1,0:T(8,128)(2,1)} %x_hbm.1, bf16[2,384,3072]{2,1,0:T(8,128)(2,1)} %wg_hbm.1, bf16[2,384,3072]{2,1,0:T(8,128)(2,1)} %wu_hbm.1, bf16[2,3072,384]{2,1,0:T(8,128)(2,1)} %wd_hbm.1), custom_call_target="tpu_custom_call" | custom-call | tf_op jit(solution)/shard_map/pallas_call | solution.py:386
  339.0 5.9 %copy.8 = bf16[2,2048,768]{2,1,0:T(8,128)(2,1)} copy(bf16[2,2048,768]{2,1,0:T(8,128)(2,1)} %shard_map.64) | data formatting | bytes 12582912

commit v3 on v2

--- a/solution.py
+++ b/solution.py
@@ -10,6 +10,7 @@
 F32 = jnp.float32
 BF16 = jnp.bfloat16
 LANES = 128
+SIGNAL_AFTER = 1
 
 
 def dot(a, b):
@@ -154,9 +155,13 @@
         base = ((g * 2 + hi) * cap).astype(F32)
         want = lax.broadcasted_iota(jnp.int32, (cap, LANES), 0).astype(F32) + base
         place = slot_buf[mb]
-        for n in range(groups):
-            p_buf[:, n * LANES:(n + 1) * LANES] = jnp.where(place[n:n + 1, :] == want, 1.0, 0.0).astype(BF16)
-        out = dot(p_buf[...], xbuf[mb]).astype(BF16)
+        out = None
+        for h in range(2):
+            for n in range(groups // 2):
+                at = h * (groups // 2) + n
+                p_buf[:, n * LANES:(n + 1) * LANES] = jnp.where(place[at:at + 1, :] == want, 1.0, 0.0).astype(BF16)
+            picked = dot(p_buf[...], xbuf[mb, h * (tok // 2):(h + 1) * (tok // 2), :])
+            out = picked if h == 0 else (out + picked).astype(BF16)
         own = home_own(i)
 
         @pl.when(own)
@@ -187,14 +192,15 @@
         return 0
 
     def wait_weights(k):
-        for c in w_local(0, k):
-            c.wait()
-        for c in w_remote(0, k):
-            c.wait()
-
-    def ffn(rows_in, k):
-        gate_pre = dot(rows_in, wg_buf[k])
-        up_pre = dot(rows_in, wu_buf[k])
+        for local, remote in zip(w_local(0, k), w_remote(0, k)):
+            local.wait()
+            remote.wait()
+
+    def pre(rows_in, k):
+        return dot(rows_in, wg_buf[k]), dot(rows_in, wu_buf[k])
+
+    def post(gate_up, k):
+        gate_pre, up_pre = gate_up
         hidden = (gate_pre / (1.0 + jnp.exp(-gate_pre)) * up_pre).astype(BF16)
         return dot(hidden, wd_buf[k])
 
@@ -203,18 +209,25 @@
         return 0
 
     def add_chunk(k, lo, hi):
-        def block(b, _):
-            oacc[b] += ffn(recv[b], k)
+        def pair(t, _):
+            both = [(t * 2 + n, pre(recv[t * 2 + n], k)) for n in range(2)]
+            for b, pre_b in both:
+                oacc[b] += post(pre_b, k)
             return 0
 
-        lax.fori_loop(lo, hi, block, 0)
+        lax.fori_loop(lax.div(lo, 2), lax.div(hi, 2), pair, 0)
 
     def finish(lo, hi):
         last = nf - 1
 
+        def slot_of(r):
+            t = lax.div(r, 2)
+            straight = 2 + lax.rem(t, 2) * 2 + lax.div(t, 2)
+            return jnp.where(is_a | (t >= 6), t, jnp.where(t < 4, straight, t - 4)), lax.rem(r, 2)
+
         def one(r, _):
-            b, sub = lax.div(r, 2), lax.rem(r, 2)
-            res = (oacc[b, part(sub), :] + ffn(recv[b, part(sub), :], last)).astype(BF16)
+            b, sub = slot_of(r)
+            res = (oacc[b, part(sub), :] + post(pre(recv[b, part(sub), :], last), last)).astype(BF16)
             own = slot_own(b, sub)
 
             @pl.when(own)
@@ -225,11 +238,11 @@
             def _():
                 recv[b, part(sub), :] = res
 
-            before = r - 1
-
-            @pl.when((r > lo * 2) & jnp.logical_not(slot_own(lax.div(before, 2), lax.rem(before, 2))))
-            def _():
-                ret_copy(lax.div(before, 2), lax.rem(before, 2)).start()
+            b_old, sub_old = slot_of(r - 1)
+
+            @pl.when((r > lo * 2) & jnp.logical_not(slot_own(b_old, sub_old)))
+            def _():
+                ret_copy(b_old, sub_old).start()
 
             return 0
 
@@ -279,14 +292,18 @@
                 add_chunk(k, lo, hi)
                 refill(k)
 
-                @pl.when((k == nf - 3) & (j == 1))
-                def _():
-                    pl.semaphore_signal(go, inc=1, device_id=device(0, 0, 1))
-
                 return 0
 
             lax.fori_loop(0, nf - 1, chunk, 0)
-            wait_weights(nf - 1)
+            last_parts = list(zip(w_local(0, nf - 1), w_remote(0, nf - 1)))
+            for n, (local, remote) in enumerate(last_parts):
+                local.wait()
+                remote.wait()
+                if n == SIGNAL_AFTER:
+                    @pl.when(j == 1)
+                    def _():
+                        pl.semaphore_signal(go, inc=1, device_id=device(0, 0, 1))
+
             finish(lo, hi)
             ret_copy(hi - 1, 1).start()
             refill(nf - 1)
@@ -322,7 +339,7 @@
 
             @pl.when(k < nf - 1)
             def _():
-                add_chunk(k, 0, 8)
+                add_chunk(k, jnp.int32(0), jnp.int32(8))
 
             @pl.when(k == early - 1)
             def _():
@@ -336,7 +353,8 @@
         finish(0, 8)
 
     def late(n, _):
-        g = lax.rem(lax.div(n, 2) + 2, 4)
+        pair = lax.div(n, 2)
+        g = jnp.where(pair < 2, pair + 2, 3 - pair)
         combine(g, lax.rem(n, 2))
         return 0
 
@@ -397,7 +415,7 @@
                 pltpu.VMEM((nf, d_model, fc), BF16),
                 pltpu.VMEM((nf, d_model, fc), BF16),
                 pltpu.VMEM((nf, fc, d_model), BF16),
-                pltpu.VMEM((cap, tok), BF16),
+                pltpu.VMEM((cap, tok // 2), BF16),
                 pltpu.VMEM((512, 2 * cap), BF16),
                 pltpu.VMEM((n_mb, groups, LANES), F32),
                 pltpu.VMEM((n_mb, LANES, LANES), F32),

time: 345 us -> 336 us (0.974)
  Pallas kernels: 339 us -> 330 us
    pallas_call x1, Pallas kernels: 339 us -> 330 us  [per_device(): pl.pallas_call(functools.partial(moe_kernel, (cap, fc, nf, early)), out_s...]
where the time goes in v3:
time: 336 us
  Pallas kernels  330 us (98%)
  local copies, waits for them, and re-layouts  5.89 us (2%)
    pallas_call x1, Pallas kernels, per_device(): pl.pallas_call(functools.partial(moe_kernel, (cap, fc, nf, early)), out_s...  330 us

profile of v3, /device:TPU:1, one launch (start us, length us, event | category | flops | bytes accessed | tf_op | source)
XLA Modules:
  0.0 336.1 jit_solution(12744647734980737004)
XLA Ops:
  0.0 330.2 %shard_map.64 = bf16[2,2048,768]{2,1,0:T(8,128)(2,1)} custom-call(s32[2,16,128]{2,1,0:T(8,128)} %bitcast.2, f32[2,16,128]{2,1,0:T(8,128)} %bitcast.3, bf16[2,2048,768]{2,1,0:T(8,128)(2,1)} %x_hbm.1, bf16[2,384,3072]{2,1,0:T(8,128)(2,1)} %wg_hbm.1, bf16[2,384,3072]{2,1,0:T(8,128)(2,1)} %wu_hbm.1, bf16[2,3072,384]{2,1,0:T(8,128)(2,1)} %wd_hbm.1), custom_call_target="tpu_custom_call" | custom-call | tf_op jit(solution)/shard_map/pallas_call | solution.py:404
  330.2 5.9 %copy.8 = bf16[2,2048,768]{2,1,0:T(8,128)(2,1)} copy(bf16[2,2048,768]{2,1,0:T(8,128)(2,1)} %shard_map.64) | data formatting | bytes 12582912

commit v4 on v3

--- a/solution.py
+++ b/solution.py
@@ -17,9 +17,9 @@
     return jnp.dot(a, b, preferred_element_type=F32)
 
 
-def moe_kernel(dims, ids_ref, gate_ref, x_hbm, wg_hbm, wu_hbm, wd_hbm, y_hbm,
+def moe_kernel(dims, ids_ref, gate_ref, x_hbm, wg_hbm, wu_hbm, wd_hbm, y_hbm, col_hbm, tail_hbm,
                xbuf, send, recv, back, oacc, wg_buf, wu_buf, wd_buf, p_buf, c_buf, slot_buf, cat_buf, col_buf,
-               x_sem, y_sem, tok_send, tok_recv, ret_send, ret_recv, w_send, w_recv, w_loc, credit, go):
+               x_sem, y_sem, col_sem, tok_send, tok_recv, ret_send, ret_recv, w_send, w_recv, w_loc, credit, go):
     cap, fc, nf, early = dims
     n_mb, tok, d_model = xbuf.shape
     half = d_model // 2
@@ -49,25 +49,40 @@
     def part(sub):
         return pl.ds(pl.multiple_of(sub * cap, cap), cap)
 
+    def send_at(i):
+        return jnp.where(i < 10, i, jnp.where(i < 12, i - 4, i - 2))
+
     def tok_copy(i):
         g, hi, mb = piece(i)
         dev = device(hi, jnp.where(g == 0, 1, 0), jnp.where(g >= 2, 0, 1))
         b = lax.rem(i, 8)
-        return pltpu.make_async_remote_copy(send.at[i], recv.at[b, part(c_me), :], tok_send.at[i],
+        return pltpu.make_async_remote_copy(send.at[send_at(i)], recv.at[b, part(c_me), :], tok_send.at[i],
                                             tok_recv.at[b * 2 + c_me], device_id=dev)
 
     def tok_arrival(b, sub):
         return pltpu.make_async_remote_copy(send.at[0], recv.at[b, part(sub), :], tok_send.at[0],
                                             tok_recv.at[b * 2 + sub], device_id=device(1, 0, 0))
 
-    def ret_copy(b, sub):
+    def ret_copy(b, sub, tail=False):
         g = (1 - c_me) * 2 + lax.div(b, 4)
         hi = 1 - lax.div(lax.rem(b, 4), 2)
         mb = lax.rem(b, 2)
         dev = device(hi, jnp.where(g == 0, 1, 0), sub)
         i = (1 - c_me) * 8 + b
-        return pltpu.make_async_remote_copy(recv.at[b, part(sub), :], back.at[g, mb, part(hi), :],
+        dst = tail_hbm if tail else back.at[g, mb, part(hi), :]
+        return pltpu.make_async_remote_copy(recv.at[b, part(sub), :], dst,
                                             ret_send.at[b * 2 + sub], ret_recv.at[i], device_id=dev)
+
+    def ret_do(b, sub, what):
+        tail = is_b & (b == 1)
+
+        @pl.when(tail)
+        def _():
+            what(ret_copy(b, sub, True))
+
+        @pl.when(jnp.logical_not(tail))
+        def _():
+            what(ret_copy(b, sub))
 
     def ret_arrival(i):
         g, hi, mb = piece(i)
@@ -170,7 +185,7 @@
 
         @pl.when(jnp.logical_not(own))
         def _():
-            send[i] = out
+            send[send_at(i)] = out
 
         @pl.when((i > 0) & jnp.logical_not(home_own(i - 1)))
         def _():
@@ -209,25 +224,35 @@
         return 0
 
     def add_chunk(k, lo, hi):
-        def pair(t, _):
-            both = [(t * 2 + n, pre(recv[t * 2 + n], k)) for n in range(2)]
+        def pair(p, _):
+            one = jnp.where(is_a, p * 2, jnp.where(p < 2, p * 6, p))
+            two = jnp.where(is_a | (p < 2), one + 1, p + 2)
+            both = [(b, pre(recv[b], k)) for b in (one, two)]
             for b, pre_b in both:
                 oacc[b] += post(pre_b, k)
             return 0
 
-        lax.fori_loop(lax.div(lo, 2), lax.div(hi, 2), pair, 0)
-
-    def finish(lo, hi):
-        last = nf - 1
-
-        def slot_of(r):
-            t = lax.div(r, 2)
-            straight = 2 + lax.rem(t, 2) * 2 + lax.div(t, 2)
-            return jnp.where(is_a | (t >= 6), t, jnp.where(t < 4, straight, t - 4)), lax.rem(r, 2)
-
+        lax.fori_loop(lo, hi, pair, 0)
+
+    def slot_of(r):
+        t = lax.div(r, 2)
+        straight = 2 + lax.rem(t, 2) * 2 + lax.div(t, 2)
+        return jnp.where(is_a | (t >= 6), t, jnp.where(t < 4, straight, t - 4)), lax.rem(r, 2)
+
+    def finish(start, lo, hi, chunks):
         def one(r, _):
+            b_old, sub_old = slot_of(r - 1)
+
+            @pl.when((r > start) & jnp.logical_not(slot_own(b_old, sub_old)))
+            def _():
+                ret_do(b_old, sub_old, lambda c: c.start())
+
             b, sub = slot_of(r)
-            res = (oacc[b, part(sub), :] + post(pre(recv[b, part(sub), :], last), last)).astype(BF16)
+            rows_in = recv[b, part(sub), :]
+            total = oacc[b, part(sub), :]
+            for k in chunks:
+                total = total + post(pre(rows_in, k), k)
+            res = total.astype(BF16)
             own = slot_own(b, sub)
 
             @pl.when(own)
@@ -238,31 +263,25 @@
             def _():
                 recv[b, part(sub), :] = res
 
-            b_old, sub_old = slot_of(r - 1)
-
-            @pl.when((r > lo * 2) & jnp.logical_not(slot_own(b_old, sub_old)))
-            def _():
-                ret_copy(b_old, sub_old).start()
-
             return 0
 
-        lax.fori_loop(lo * 2, hi * 2, one, 0)
-
-    def combine(g, mb):
-        for hi in range(2):
+        lax.fori_loop(lo, hi, one, 0)
+
+    def combine(g, mb, width=2 * cap):
+        for hi in range(width // cap):
             i = g * 4 + (1 - hi) * 2 + mb
 
             @pl.when(jnp.logical_not(home_own(i)))
             def _():
                 ret_arrival(i).wait_recv()
 
-        want = lax.broadcasted_iota(jnp.int32, (LANES, 2 * cap), 1).astype(F32) + (g * 2 * cap).astype(F32)
+        want = lax.broadcasted_iota(jnp.int32, (LANES, width), 1).astype(F32) + (g * 2 * cap).astype(F32)
         size = c_buf.shape[0]
         for blk in range(tok // size):
             for s in range(size // LANES):
                 n = blk * (size // LANES) + s
-                c_buf[s * LANES:(s + 1) * LANES, :] = jnp.where(col_buf[mb, :, n:n + 1] == want, 1.0, 0.0).astype(BF16)
-            picked = dot(c_buf[...], back[g, mb])
+                c_buf[s * LANES:(s + 1) * LANES, 0:width] = jnp.where(col_buf[mb, :, n:n + 1] == want, 1.0, 0.0).astype(BF16)
+            picked = dot(c_buf[:, 0:width], back[g, mb, 0:width, :])
             for s in range(size // LANES):
                 n = blk * (size // LANES) + s
                 at = slice(n * LANES, (n + 1) * LANES)
@@ -289,7 +308,7 @@
 
             def chunk(k, _):
                 wait_weights(k)
-                add_chunk(k, lo, hi)
+                add_chunk(k, j * 2, j * 2 + 2)
                 refill(k)
 
                 return 0
@@ -304,7 +323,7 @@
                     def _():
                         pl.semaphore_signal(go, inc=1, device_id=device(0, 0, 1))
 
-            finish(lo, hi)
+            finish(lo * 2, lo * 2, hi * 2, (nf - 1,))
             ret_copy(hi - 1, 1).start()
             refill(nf - 1)
             return 0
@@ -339,7 +358,7 @@
 
             @pl.when(k < nf - 1)
             def _():
-                add_chunk(k, jnp.int32(0), jnp.int32(8))
+                add_chunk(k, 0, jnp.where(k == nf - 2, 3, 4))
 
             @pl.when(k == early - 1)
             def _():
@@ -350,7 +369,9 @@
             return 0
 
         lax.fori_loop(0, nf, chunk, 0)
-        finish(0, 8)
+        finish(0, 0, 4, (nf - 1,))
+        finish(0, 4, 8, (nf - 2, nf - 1))
+        finish(0, 8, 16, (nf - 1,))
 
     def late(n, _):
         pair = lax.div(n, 2)
@@ -358,11 +379,16 @@
         combine(g, lax.rem(n, 2))
         return 0
 
-    lax.fori_loop(2 * c_me, 7, late, 0)
+    lax.fori_loop(2 * c_me, 6, late, 0)
     outs = [pltpu.make_async_copy(xbuf.at[mb], y_hbm.at[mb], y_sem.at[mb]) for mb in range(n_mb)]
+    col_out = pltpu.make_async_copy(col_buf.at[1], col_hbm, col_sem)
+    combine(jnp.int32(0), jnp.int32(1), cap)
+    outs[1].start()
+    col_out.start()
+    combine(jnp.int32(0), jnp.int32(0))
     outs[0].start()
-    late(jnp.int32(7), 0)
-    outs[1].start()
+    pltpu.make_async_remote_copy(send.at[0], tail_hbm, ret_send.at[0], ret_recv.at[1],
+                                 device_id=device(1, 0, 0)).wait_recv()
 
     def drain(i, _):
         @pl.when(jnp.logical_not(home_own(i)))
@@ -373,13 +399,57 @@
 
         @pl.when(jnp.logical_not(slot_own(b, sub)))
         def _():
-            ret_copy(b, sub).wait_send()
+            ret_do(b, sub, lambda c: c.wait_send())
 
         return 0
 
     lax.fori_loop(0, 16, drain, 0)
-    for c in outs:
+    for c in outs + [col_out]:
         c.wait()
+
+
+def tail_kernel(cap, y_hbm, col_hbm, tail_hbm, out_hbm, buf, col, tail, c_buf, in_sem, out_sem, col_sem, tail_sem):
+    n_mb, tok, _ = buf.shape
+    parts = 4
+    size = tok // parts
+    per = size // LANES
+    groups = tok // LANES
+    loads = [pltpu.make_async_copy(col_hbm, col, col_sem), pltpu.make_async_copy(tail_hbm, tail, tail_sem)]
+    for c in loads:
+        c.start()
+
+    def rows_at(p):
+        return p // parts, pl.ds((p % parts) * size, size)
+
+    def move(p, out):
+        mb, at = rows_at(p)
+        if out:
+            return pltpu.make_async_copy(buf.at[mb, at, :], out_hbm.at[mb, at, :], out_sem.at[p])
+        return pltpu.make_async_copy(y_hbm.at[mb, at, :], buf.at[mb, at, :], in_sem.at[p])
+
+    for p in range(n_mb * parts):
+        move(p, False).start()
+    loads[0].wait()
+    want = lax.broadcasted_iota(jnp.int32, (LANES, cap), 1).astype(F32) + float(cap)
+    for n in range(groups):
+        c_buf[n * LANES:(n + 1) * LANES, :] = jnp.where(col[:, n:n + 1] == want, 1.0, 0.0).astype(BF16)
+    loads[1].wait()
+    for p in range(parts):
+        move(p, False).wait()
+        move(p, True).start()
+    for p in range(parts, 2 * parts):
+        blk = p - parts
+        picked = dot(c_buf[blk * size:(blk + 1) * size, :], tail[...])
+        move(p, False).wait()
+        for s in range(per):
+            n = blk * per + s
+            at = slice(n * LANES, (n + 1) * LANES)
+            gate = col[:, groups + n:groups + n + 1]
+            part = picked[s * LANES:(s + 1) * LANES, :]
+            buf[1, at, :] = (buf[1, at, :].astype(F32) + gate * part).astype(BF16)
+        move(p, True).start()
+    for p in range(2 * parts):
+        move(p, True).wait()
 
 
 def solution(mesh):
@@ -396,19 +466,20 @@
         cap = 8 * ((5 * n_top * tok + 32 * n_exp - 1) // (32 * n_exp))
         fc = 256
         nf = ff // fc
-        early = 9
+        early = 8
         groups = tok // LANES
         hbm = pl.BlockSpec(memory_space=pl.ANY)
         vmem = pl.BlockSpec(memory_space=pltpu.VMEM)
         dma = pltpu.SemaphoreType.DMA
-        return pl.pallas_call(
+        y_part, col, tail = pl.pallas_call(
             functools.partial(moe_kernel, (cap, fc, nf, early)),
-            out_shape=jax.ShapeDtypeStruct(x_loc.shape, BF16),
+            out_shape=(jax.ShapeDtypeStruct(x_loc.shape, BF16), jax.ShapeDtypeStruct((LANES, LANES), F32),
+                       jax.ShapeDtypeStruct((cap, d_model), BF16)),
             in_specs=[vmem, vmem, hbm, hbm, hbm, hbm],
-            out_specs=hbm,
+            out_specs=(hbm, hbm, hbm),
             scratch_shapes=[
                 pltpu.VMEM((n_mb, tok, d_model), BF16),
-                pltpu.VMEM((16, cap, d_model), BF16),
+                pltpu.VMEM((14, cap, d_model), BF16),
                 pltpu.VMEM((8, 2 * cap, d_model), BF16),
                 pltpu.VMEM((4, n_mb, 2 * cap, d_model), BF16),
                 pltpu.VMEM((8, 2 * cap, d_model), F32),
@@ -420,7 +491,7 @@
                 pltpu.VMEM((n_mb, groups, LANES), F32),
                 pltpu.VMEM((n_mb, LANES, LANES), F32),
                 pltpu.VMEM((n_mb, LANES, LANES), F32),
-                dma((n_mb,)), dma((n_mb,)),
+                dma((n_mb,)), dma((n_mb,)), dma,
                 dma((16,)), dma((16,)), dma((16,)), dma((16,)),
                 dma((nf, 3)), dma((nf, 3)), dma((nf, 3)),
                 pltpu.SemaphoreType.REGULAR, pltpu.SemaphoreType.REGULAR,
@@ -428,6 +499,16 @@
             compiler_params=pltpu.CompilerParams(
                 collective_id=0, has_side_effects=True, vmem_limit_bytes=64 * 1024 * 1024 - 65536),
         )(idx_loc.reshape(n_mb, groups, LANES), gate_loc.reshape(n_mb, groups, LANES), x_loc, wg_loc, wu_loc, wd_loc)
+        return pl.pallas_call(
+            functools.partial(tail_kernel, cap),
+            out_shape=jax.ShapeDtypeStruct(x_loc.shape, BF16),
+            in_specs=[hbm, hbm, hbm],
+            out_specs=hbm,
+            scratch_shapes=[
+                pltpu.VMEM((n_mb, tok, d_model), BF16), pltpu.VMEM((LANES, LANES), F32), pltpu.VMEM((cap, d_model), BF16),
+                pltpu.VMEM((tok, cap), BF16), dma((8,)), dma((8,)), dma, dma,
+            ],
+        )(y_part, col, tail)
 
     return jax.shard_map(per_device, mesh=mesh, in_specs=(row_spec, row_spec, row_spec, up_spec, up_spec, down_spec),
                          out_specs=row_spec, check_vma=False)

time: 336 us -> 332 us (0.988)
  local copies, waits for them, and re-layouts: 5.89 us -> 0 us
    pallas_call x0 -> x1, Pallas kernels: none -> 6.99 us  [per_device(): pl.pallas_call(functools.partial(tail_kernel, cap), out_shape=jax.ShapeDt...]
    pallas_call x1, Pallas kernels: 330 us -> 324 us  [per_device(): pl.pallas_call(functools.partial(moe_kernel, (cap, fc, nf, early)), out_s...]
    unnamed x1 -> x0, local copies, waits for them, and re-layouts: 5.89 us -> none
where the time goes in v4:
time: 332 us; the launch traced here: 331 us
  Pallas kernels  331 us (100%)
    pallas_call x1, Pallas kernels, per_device(): pl.pallas_call(functools.partial(moe_kernel, (cap, fc, nf, early)), out_s...  324 us
    pallas_call x1, Pallas kernels, per_device(): pl.pallas_call(functools.partial(tail_kernel, cap), out_shape=jax.ShapeDt...  6.99 us

profile of v4, /device:TPU:1, one launch (start us, length us, event | category | flops | bytes accessed | tf_op | source)
XLA Modules:
  0.0 331.4 jit_solution(14390680077330422879)
XLA Ops:
  0.0 324.2 %shard_map.64 = (bf16[2,2048,768]{2,1,0:T(8,128)(2,1)}, f32[128,128]{1,0:T(8,128)}, bf16[320,768]{1,0:T(8,128)(2,1)}) custom-call(s32[2,16,128]{2,1,0:T(8,128)} %bitcast.2, f32[2,16,128]{2,1,0:T(8,128)} %bitcast.3, bf16[2,2048,768]{2,1,0:T(8,128)(2,1)} %x_hbm.1, bf16[2,384,3072]{2,1,0:T(8,128)(2,1)} %wg_hbm.1, bf16[2,384,3072]{2,1,0:T(8,128)(2,1)} %wu_hbm.1, ...), custom_call_target="tpu_custom_call" | custom-call | tf_op jit(solution)/shard_map/pallas_call | solution.py:474
  324.2 7.0 %shard_map.65 = bf16[2,2048,768]{2,1,0:T(8,128)(2,1)} custom-call(bf16[2,2048,768]{2,1,0:T(8,128)(2,1)} %get-tuple-element.8.y_hbm, f32[128,128]{1,0:T(8,128)} %get-tuple-element.9.col_hbm, bf16[320,768]{1,0:T(8,128)(2,1)} %get-tuple-element.10.tail_hbm), custom_call_target="tpu_custom_call" | custom-call | tf_op jit(solution)/shard_map/pallas_call | solution.py:502

commit v5 on v4

--- a/solution.py
+++ b/solution.py
@@ -17,9 +17,9 @@
     return jnp.dot(a, b, preferred_element_type=F32)
 
 
-def moe_kernel(dims, ids_ref, gate_ref, x_hbm, wg_hbm, wu_hbm, wd_hbm, y_hbm, col_hbm, tail_hbm,
-               xbuf, send, recv, back, oacc, wg_buf, wu_buf, wd_buf, p_buf, c_buf, slot_buf, cat_buf, col_buf,
-               x_sem, y_sem, col_sem, tok_send, tok_recv, ret_send, ret_recv, w_send, w_recv, w_loc, credit, go):
+def moe_kernel(dims, ids_hbm, gate_hbm, x_hbm, wg_hbm, wu_hbm, wd_hbm, y_hbm, col_hbm, tail_hbm,
+               ids_ref, gate_ref, h_buf, xbuf, send, recv, back, oacc, wg_buf, wu_buf, wd_buf, p_buf, c_buf, slot_buf, cat_buf, col_buf,
+               in_sem, x_sem, y_sem, col_sem, tok_send, tok_recv, ret_send, ret_recv, w_send, w_recv, w_loc, credit, go):
     cap, fc, nf, early = dims
     n_mb, tok, d_model = xbuf.shape
     half = d_model // 2
@@ -125,11 +125,16 @@
         return 0
 
     lax.fori_loop(0, early * c_me, start_remote, 0)
+    small = [pltpu.make_async_copy(ids_hbm, ids_ref, in_sem.at[0]), pltpu.make_async_copy(gate_hbm, gate_ref, in_sem.at[1])]
+    for c in small:
+        c.start()
     x_loads = [pltpu.make_async_copy(x_hbm.at[mb], xbuf.at[mb], x_sem.at[mb]) for mb in range(n_mb)]
     for c in x_loads:
         c.start()
     lax.fori_loop(0, nf, start_local, 0)
 
+    for c in small:
+        c.wait()
     masks = []
     for mb in range(n_mb):
         ids = ids_ref[mb]
@@ -214,10 +219,12 @@
     def pre(rows_in, k):
         return dot(rows_in, wg_buf[k]), dot(rows_in, wu_buf[k])
 
+    def hidden(gate_up):
+        gate_pre, up_pre = gate_up
+        return (gate_pre / (1.0 + jnp.exp(-gate_pre)) * up_pre).astype(BF16)
+
     def post(gate_up, k):
-        gate_pre, up_pre = gate_up
-        hidden = (gate_pre / (1.0 + jnp.exp(-gate_pre)) * up_pre).astype(BF16)
-        return dot(hidden, wd_buf[k])
+        return dot(hidden(gate_up), wd_buf[k])
 
     def clear(b, _):
         oacc[b] = jnp.zeros_like(oacc[b])
@@ -239,7 +246,7 @@
         straight = 2 + lax.rem(t, 2) * 2 + lax.div(t, 2)
         return jnp.where(is_a | (t >= 6), t, jnp.where(t < 4, straight, t - 4)), lax.rem(r, 2)
 
-    def finish(start, lo, hi, chunks):
+    def finish(start, lo, hi, chunks, ready=False):
         def one(r, _):
             b_old, sub_old = slot_of(r - 1)
 
@@ -250,6 +257,8 @@
             b, sub = slot_of(r)
             rows_in = recv[b, part(sub), :]
             total = oacc[b, part(sub), :]
+            if ready:
+                total = total + dot(h_buf[part(sub), :], wd_buf[nf - 1])
             for k in chunks:
                 total = total + post(pre(rows_in, k), k)
             res = total.astype(BF16)
@@ -356,9 +365,7 @@
                 for c in w_remote(0, k):
                     c.wait_send()
 
-            @pl.when(k < nf - 1)
-            def _():
-                add_chunk(k, 0, jnp.where(k == nf - 2, 3, 4))
+            add_chunk(k, 0, jnp.where(k == nf - 2, 3, 4))
 
             @pl.when(k == early - 1)
             def _():
@@ -368,8 +375,14 @@
 
             return 0
 
-        lax.fori_loop(0, nf, chunk, 0)
-        finish(0, 0, 4, (nf - 1,))
+        lax.fori_loop(0, nf - 1, chunk, 0)
+        for n, (local, remote) in enumerate(zip(w_local(0, nf - 1), w_remote(0, nf - 1))):
+            local.wait()
+            remote.wait()
+            if n == 1:
+                h_buf[...] = hidden(pre(recv[2], nf - 1))
+        finish(0, 0, 2, (), ready=True)
+        finish(0, 2, 4, (nf - 1,))
         finish(0, 4, 8, (nf - 2, nf - 1))
         finish(0, 8, 16, (nf - 1,))
 
@@ -469,15 +482,16 @@
         early = 8
         groups = tok // LANES
         hbm = pl.BlockSpec(memory_space=pl.ANY)
-        vmem = pl.BlockSpec(memory_space=pltpu.VMEM)
         dma = pltpu.SemaphoreType.DMA
         y_part, col, tail = pl.pallas_call(
             functools.partial(moe_kernel, (cap, fc, nf, early)),
             out_shape=(jax.ShapeDtypeStruct(x_loc.shape, BF16), jax.ShapeDtypeStruct((LANES, LANES), F32),
                        jax.ShapeDtypeStruct((cap, d_model), BF16)),
-            in_specs=[vmem, vmem, hbm, hbm, hbm, hbm],
+            in_specs=[hbm] * 6,
             out_specs=(hbm, hbm, hbm),
             scratch_shapes=[
+                pltpu.VMEM((n_mb, groups, LANES), jnp.int32), pltpu.VMEM((n_mb, groups, LANES), F32),
+                pltpu.VMEM((2 * cap, fc), BF16),
                 pltpu.VMEM((n_mb, tok, d_model), BF16),
                 pltpu.VMEM((14, cap, d_model), BF16),
                 pltpu.VMEM((8, 2 * cap, d_model), BF16),
@@ -491,7 +505,7 @@
                 pltpu.VMEM((n_mb, groups, LANES), F32),
                 pltpu.VMEM((n_mb, LANES, LANES), F32),
                 pltpu.VMEM((n_mb, LANES, LANES), F32),
-                dma((n_mb,)), dma((n_mb,)), dma,
+                dma((2,)), dma((n_mb,)), dma((n_mb,)), dma,
                 dma((16,)), dma((16,)), dma((16,)), dma((16,)),
                 dma((nf, 3)), dma((nf, 3)), dma((nf, 3)),
                 pltpu.SemaphoreType.REGULAR, pltpu.SemaphoreType.REGULAR,

time: 332 us -> 331 us (level)
  no operation moved by 1% of the time
where the time goes in v5:
time: 331 us
  Pallas kernels  330 us (100%)
    pallas_call x1, Pallas kernels, per_device(): pl.pallas_call(functools.partial(moe_kernel, (cap, fc, nf, early)), out_s...  323 us
    pallas_call x1, Pallas kernels, per_device(): pl.pallas_call(functools.partial(tail_kernel, cap), out_shape=jax.ShapeDt...  7 us

profile of v5, /device:TPU:1, one launch (start us, length us, event | category | flops | bytes accessed | tf_op | source)
XLA Modules:
  0.0 330.5 jit_solution(13563801497036460410)
XLA Ops:
  0.0 323.3 %shard_map.64 = (bf16[2,2048,768]{2,1,0:T(8,128)(2,1)}, f32[128,128]{1,0:T(8,128)}, bf16[320,768]{1,0:T(8,128)(2,1)}) custom-call(s32[2,16,128]{2,1,0:T(8,128)} %bitcast.2, f32[2,16,128]{2,1,0:T(8,128)} %bitcast.3, bf16[2,2048,768]{2,1,0:T(8,128)(2,1)} %x_hbm.1, bf16[2,384,3072]{2,1,0:T(8,128)(2,1)} %wg_hbm.1, bf16[2,384,3072]{2,1,0:T(8,128)(2,1)} %wu_hbm.1, ...), custom_call_target="tpu_custom_call" | custom-call | tf_op jit(solution)/shard_map/pallas_call | solution.py:486
  323.4 7.0 %shard_map.65 = bf16[2,2048,768]{2,1,0:T(8,128)(2,1)} custom-call(bf16[2,2048,768]{2,1,0:T(8,128)(2,1)} %get-tuple-element.8.y_hbm, f32[128,128]{1,0:T(8,128)} %get-tuple-element.9.col_hbm, bf16[320,768]{1,0:T(8,128)(2,1)} %get-tuple-element.10.tail_hbm), custom_call_target="tpu_custom_call" | custom-call | tf_op jit(solution)/shard_map/pallas_call | solution.py:516

commit v6 on v5

--- a/solution.py
+++ b/solution.py
@@ -365,7 +365,7 @@
                 for c in w_remote(0, k):
                     c.wait_send()
 
-            add_chunk(k, 0, jnp.where(k == nf - 2, 3, 4))
+            add_chunk(k, jnp.where(k == nf - 2, 1, 0), jnp.where(k == nf - 2, 3, 4))
 
             @pl.when(k == early - 1)
             def _():
@@ -383,8 +383,8 @@
                 h_buf[...] = hidden(pre(recv[2], nf - 1))
         finish(0, 0, 2, (), ready=True)
         finish(0, 2, 4, (nf - 1,))
-        finish(0, 4, 8, (nf - 2, nf - 1))
-        finish(0, 8, 16, (nf - 1,))
+        finish(0, 4, 12, (nf - 2, nf - 1))
+        finish(0, 12, 16, (nf - 1,))
 
     def late(n, _):
         pair = lax.div(n, 2)

time: 331 us -> 329 us (level)
  no operation moved by 1% of the time
where the time goes in v6:
time: 329 us
  Pallas kernels  329 us (100%)
    pallas_call x1, Pallas kernels, per_device(): pl.pallas_call(functools.partial(moe_kernel, (cap, fc, nf, early)), out_s...  322 us
    pallas_call x1, Pallas kernels, per_device(): pl.pallas_call(functools.partial(tail_kernel, cap), out_shape=jax.ShapeDt...  6.99 us

profile of v6, /device:TPU:1, one launch (start us, length us, event | category | flops | bytes accessed | tf_op | source)
XLA Modules:
  0.0 329.1 jit_solution(13261962450828010276)
XLA Ops:
  0.0 322.0 %shard_map.64 = (bf16[2,2048,768]{2,1,0:T(8,128)(2,1)}, f32[128,128]{1,0:T(8,128)}, bf16[320,768]{1,0:T(8,128)(2,1)}) custom-call(s32[2,16,128]{2,1,0:T(8,128)} %bitcast.2, f32[2,16,128]{2,1,0:T(8,128)} %bitcast.3, bf16[2,2048,768]{2,1,0:T(8,128)(2,1)} %x_hbm.1, bf16[2,384,3072]{2,1,0:T(8,128)(2,1)} %wg_hbm.1, bf16[2,384,3072]{2,1,0:T(8,128)(2,1)} %wu_hbm.1, ...), custom_call_target="tpu_custom_call" | custom-call | tf_op jit(solution)/shard_map/pallas_call | solution.py:486
  322.0 7.0 %shard_map.65 = bf16[2,2048,768]{2,1,0:T(8,128)(2,1)} custom-call(bf16[2,2048,768]{2,1,0:T(8,128)(2,1)} %get-tuple-element.8.y_hbm, f32[128,128]{1,0:T(8,128)} %get-tuple-element.9.col_hbm, bf16[320,768]{1,0:T(8,128)(2,1)} %get-tuple-element.10.tail_hbm), custom_call_target="tpu_custom_call" | custom-call | tf_op jit(solution)/shard_map/pallas_call | solution.py:516
